TPU v7x, 32 devices: a whole 2x2x4 slice. The times are simulated.
32 devices in a mesh: groups: 2 (over y), block: 4 (over z), seg: 2 (over x), sub: 2 (over core).
Axes of the slice: x: 2, y: 2, z: 4, core: 2. Of those that a mesh axis runs over, the one named last changes fastest.
Arguments:
- old_fields: float32 [2048, 4, 512], P(('groups', 'block', 'seg', 'sub')), parts along dimension 0, may hold values from -6 to 6
- corner_shift: float32 [24, 2048], P(None, ('groups', 'block', 'seg', 'sub')), parts along dimension 1, may hold values from -0.2 to 0.2
- targets: float32 [3, 131072], P(None, ('groups', 'block', 'seg', 'sub')), parts along dimension 1, may hold values from -0.7 to 0.7
- owners: int32 [1024], P(('groups', 'block', 'seg', 'sub')), parts along dimension 0, may hold values from 0 to 1023, as said below
Outputs:
- new_fields: float32 [4, 131072], P(None, ('groups', 'block', 'seg', 'sub')), parts along dimension 1
There are 2 independent parts, one for each index of `groups`. A program takes and returns all parts, laid end to end along the dimension named above; each array names one. Nothing has to cross between parts.
Inputs may be any that keep to these rules, and one draw needn't show every extreme that they name: `owners`: owner e lies on device e // 64. At most 2 of the blocks on the rows of one device are owned by elements of any one device, and in every draw some device owns exactly 2 blocks of every device.
All inputs are finite; a program needn't handle non-finite values.
Results may differ from a plain program's by a relative error of at most 0.00029.
Values sent between devices are 32-bit elements; how exact they have to be, the bound alone decides.
A program may use at most 64 MiB of HBM per device.

v0:
```python
import jax
import jax.numpy as jnp
import numpy as np
from jax import lax
from jax.sharding import PartitionSpec as P

NEWTON = 3
CAP = 2
GLL_POINTS = (
    -1.0,
    -0.8717401485096066,
    -0.5917001814331423,
    -0.2092992179024789,
    0.2092992179024789,
    0.5917001814331423,
    0.8717401485096066,
    1.0,
)
EXACT = lax.Precision.HIGHEST


def lagrange_rows(coords):
    gll_nodes = jnp.array(GLL_POINTS, jnp.float32)
    offsets = coords[None, :] - gll_nodes[:, None]
    spacing = gll_nodes[:, None] - gll_nodes[None, :] + jnp.eye(8, dtype=jnp.float32)
    diag_mask = jnp.eye(8, dtype=bool)
    factors = jnp.where(diag_mask[:, :, None], 1.0, offsets[None, :, :] / spacing[:, :, None])
    return jnp.prod(factors, axis=1)


def corner_signs():
    bit_table = np.array(
        [[corner >> 2 - coord_dim & 1 for corner in range(8)] for coord_dim in range(3)], np.float32
    )
    return jnp.asarray(2.0 * bit_table - 1.0)


def outer_prod(first, second, third):
    return (first[:, None, None, :] * second[None, :, None, :] * third[None, None, :, :]).reshape(
        8, -1
    )


def trilinear(ref_pos):
    shape_list = []
    slope_list = []
    for coord_dim in range(3):
        coordinate = ref_pos[coord_dim]
        shape_list.append(jnp.stack([0.5 - 0.5 * coordinate, 0.5 + 0.5 * coordinate]))
        slope_list.append(
            jnp.stack([jnp.full_like(coordinate, -0.5), jnp.full_like(coordinate, 0.5)])
        )
    values = outer_prod(shape_list[0], shape_list[1], shape_list[2])
    slopes = [
        outer_prod(slope_list[0], shape_list[1], shape_list[2]),
        outer_prod(shape_list[0], slope_list[1], shape_list[2]),
        outer_prod(shape_list[0], shape_list[1], slope_list[2]),
    ]
    return (values, slopes)


def solve_three(matrix, rhs_rows):
    cofactors = []
    for row_id in range(3):
        keep_rows = [remain for remain in range(3) if remain != row_id]
        cof_row = []
        for col_id in range(3):
            keep_cols = [remain for remain in range(3) if remain != col_id]
            sign_factor = 1.0 if (row_id + col_id) % 2 == 0 else -1.0
            cof_row.append(
                sign_factor
                * (
                    matrix[keep_rows[0]][keep_cols[0]] * matrix[keep_rows[1]][keep_cols[1]]
                    - matrix[keep_rows[0]][keep_cols[1]] * matrix[keep_rows[1]][keep_cols[0]]
                )
            )
        cofactors.append(cof_row)
    determinant = (
        matrix[0][0] * cofactors[0][0]
        + matrix[0][1] * cofactors[0][1]
        + matrix[0][2] * cofactors[0][2]
    )
    return [
        (
            cofactors[0][col_id] * rhs_rows[0]
            + cofactors[1][col_id] * rhs_rows[1]
            + cofactors[2][col_id] * rhs_rows[2]
        )
        / determinant
        for col_id in range(3)
    ]


def invert_map(corners, target):
    ref_pos = jnp.zeros_like(target)
    for iteration in range(NEWTON):
        values, slopes = trilinear(ref_pos)
        mapped = jnp.dot(corners, values, precision=EXACT)
        columns = [jnp.dot(corners, slope_row, precision=EXACT) for slope_row in slopes]
        matrix = [[columns[col_id][row_id] for col_id in range(3)] for row_id in range(3)]
        misfit = mapped - target
        update = solve_three(matrix, [misfit[row_id] for row_id in range(3)])
        ref_pos = jnp.clip(ref_pos - jnp.stack(update), -1.2, 1.2)
    return ref_pos


def interpolate(element_field, corners, target):
    ref_pos = invert_map(corners, target)
    along_x = lagrange_rows(ref_pos[0])
    along_y = lagrange_rows(ref_pos[1])
    along_z = lagrange_rows(ref_pos[2])
    weights = (along_y[:, None, :] * along_z[None, :, :]).reshape(64, -1)
    var_count = element_field.shape[0]
    partial_sum = jnp.dot(element_field.reshape(var_count * 8, 64), weights, precision=EXACT)
    return jnp.sum(partial_sum.reshape(var_count, 8, -1) * along_x[None, :, :], axis=1)


def interpolate_blocks(fields, shifts, points):
    cube_signs = corner_signs()

    def per_block(inputs):
        element_field, shift_row, target = inputs
        return interpolate(element_field, cube_signs + shift_row.reshape(3, 8), target)

    return lax.map(per_block, (fields, shifts, points), batch_size=64)


def slot_table(owners, elems_local, capacity):
    owner_dev = owners // elems_local
    local_elem = owners - owner_dev * elems_local
    block_count = owners.shape[0]
    earlier = jnp.tril(jnp.ones((block_count, block_count), jnp.int32), -1)
    matches = (owner_dev[:, None] == owner_dev[None, :]).astype(jnp.int32)
    arrival = jnp.sum(matches * earlier, axis=1)
    return (owner_dev * capacity + arrival, local_elem)


def shards(old_fields, corner_shift, targets, owners):
    outer_count = lax.axis_size("block")
    inner_count = lax.axis_size("seg") * lax.axis_size("sub")
    slot_count = outer_count * inner_count * CAP
    elems_local = old_fields.shape[0]
    var_count = old_fields.shape[1]
    block_count = owners.shape[0]
    slot_index, local_elem = slot_table(owners, elems_local, CAP)
    block_points = targets.reshape(3, block_count, -1).transpose(1, 0, 2)
    point_count = block_points.shape[2]
    outgoing = jnp.zeros((slot_count, 3, point_count), jnp.float32).at[slot_index].set(block_points)
    wanted = jnp.full((slot_count,), -1, jnp.int32).at[slot_index].set(local_elem)
    arrived, asked = (
        lax.all_to_all(
            lax.all_to_all(
                outgoing.reshape(outer_count, inner_count, CAP, 3, point_count),
                "block",
                split_axis=0,
                concat_axis=0,
                tiled=True,
            ),
            ("seg", "sub"),
            split_axis=1,
            concat_axis=1,
            tiled=True,
        ),
        lax.all_to_all(
            lax.all_to_all(
                wanted.reshape(outer_count, inner_count, CAP),
                "block",
                split_axis=0,
                concat_axis=0,
                tiled=True,
            ),
            ("seg", "sub"),
            split_axis=1,
            concat_axis=1,
            tiled=True,
        ),
    )
    asked = asked.reshape(slot_count)
    live_slot = asked >= 0
    element = jnp.where(live_slot, asked, 0)
    fields = old_fields[element]
    shifts = jnp.transpose(corner_shift[:, element])
    computed = interpolate_blocks(fields, shifts, arrived.reshape(slot_count, 3, point_count))
    computed = jnp.where(live_slot[:, None, None], computed, 0.0)
    returned = lax.all_to_all(
        lax.all_to_all(
            computed.reshape(outer_count, inner_count, CAP, var_count, point_count),
            "block",
            split_axis=0,
            concat_axis=0,
            tiled=True,
        ),
        ("seg", "sub"),
        split_axis=1,
        concat_axis=1,
        tiled=True,
    )
    mine = returned.reshape(slot_count, var_count, point_count)[slot_index]
    return mine.transpose(1, 0, 2).reshape(var_count, -1)


def solution(mesh):
    in_specs = (
        P(("groups", "block", "seg", "sub"), None, None),
        P(None, ("groups", "block", "seg", "sub")),
        P(None, ("groups", "block", "seg", "sub")),
        P(("groups", "block", "seg", "sub")),
    )
    out_specs = P(None, ("groups", "block", "seg", "sub"))
    return jax.shard_map(shards, mesh=mesh, in_specs=in_specs, out_specs=out_specs, check_vma=False)
```

profile of v0, /device:TPU:0, one launch (start us, length us, event | category | flops | bytes accessed | tf_op | source)
XLA Modules:
  0.0 64.6 jit_solution(12692678252523733216)
XLA Ops:
  0.0 0.7 %multiply_subtract_fusion.2 = (s32[32]{0:T(128)S(1)}, s32[32]{0:T(128)S(1)}, s32[32]{0:T(128)S(1)}) fusion(s32[32]{0:T(128)} %param.11), kind=kLoop, calls=%fused_computation.237 | loop fusion | flops 576 | bytes 512 | tf_op jit(solution)/shard_map/sub | solution.py:130
  0.7 0.2 select_reduce_fusion
  0.9 0.7 %scatter_custom_fusion = s32[32]{0:T(128)S(1)} fusion(s32[32]{0:T(128)S(1)} %compare_select_fusion.2, s32[32]{0:T(128)S(1)} %get-tuple-element.10, s32[]{:T(128)} %constant.26.clone.1), kind=kCustom, calls=%fused_computation.239 | custom fusion | bytes 132 | tf_op jit(solution)/shard_map/scatter | solution.py:149
  1.7 0.7 %copy.272 = s32[4,4,2]{1,2,0:T(2,128)} copy(s32[4,4,2]{2,1,0:T(4,128)S(1)} %reshape.2161) | data formatting | bytes 256 | tf_op jit(solution)/shard_map/reshape | solution.py:166
  2.4 6.5 %all-to-all-start = ((s32[4,4,2]{1,2,0:T(2,128)}), s32[4,4,2]{1,2,0:T(2,128)S(1)}, u32[]{:S(2)}, u32[]{:S(2)}) async-start(s32[4,4,2]{1,2,0:T(2,128)} %copy.272), calls=%async_computation | async-start | bytes 8192 | tf_op jit(solution)/shard_map/all_to_all | solution.py:165
  9.1 1.5 %scatter_fusion = f32[32,3,128]{2,1,0:T(4,128)S(1)} fusion(f32[32,3,128]{2,1,0:T(4,128)S(1)} %broadcast.569, s32[32]{0:T(128)S(1)} %compare_select_fusion.2, f32[32,3,128]{2,1,0:T(4,128)S(1)} %bitcast.790), kind=kCustom, calls=%fused_computation.4 | custom fusion | bytes 147584 | tf_op jit(solution)/shard_map/scatter | solution.py:148
  10.6 3.9 %all-to-all-done = s32[4,4,2]{1,2,0:T(2,128)S(1)} async-done(((s32[4,4,2]{1,2,0:T(2,128)}), s32[4,4,2]{1,2,0:T(2,128)S(1)}, u32[]{:S(2)}, u32[]{:S(2)}) %all-to-all-start) | async-done | bytes 160 | tf_op jit(solution)/shard_map/all_to_all | solution.py:165
  14.5 0.7 %copy.273 = s32[4,4,2]{0,2,1:T(2,128)} copy(s32[4,4,2]{1,2,0:T(2,128)S(1)} %all-to-all-done) | data formatting | bytes 256 | tf_op jit(solution)/shard_map/all_to_all | solution.py:165
  15.2 3.2 %all-to-all-start.1 = ((s32[4,4,2]{0,2,1:T(2,128)}), s32[4,4,2]{0,2,1:T(2,128)S(1)}, u32[]{:S(2)}, u32[]{:S(2)}) async-start(s32[4,4,2]{0,2,1:T(2,128)} %copy.273), calls=%async_computation.1 | async-start | bytes 8192 | tf_op jit(solution)/shard_map/all_to_all | solution.py:164
  18.4 0.6 %copy.281 = f32[4,4,2,3,128]{4,2,1,3,0:T(2,128)} copy(f32[4,4,2,3,128]{4,3,2,1,0:T(4,128)S(1)} %bitcast.767) | data formatting | bytes 98304 | tf_op jit(solution)/shard_map/reshape | solution.py:153
  19.1 3.1 %all-to-all-done.1 = s32[4,4,2]{0,2,1:T(2,128)S(1)} async-done(((s32[4,4,2]{0,2,1:T(2,128)}), s32[4,4,2]{0,2,1:T(2,128)S(1)}, u32[]{:S(2)}, u32[]{:S(2)}) %all-to-all-start.1) | async-done | bytes 160 | tf_op jit(solution)/shard_map/all_to_all | solution.py:164
  22.2 3.3 %all-to-all-start.2 = ((f32[4,4,2,3,128]{4,2,1,3,0:T(2,128)}), f32[4,4,2,3,128]{4,2,1,3,0:T(2,128)S(1)}, u32[]{:S(2)}, u32[]{:S(2)}) async-start(f32[4,4,2,3,128]{4,2,1,3,0:T(2,128)} %copy.281), calls=%async_computation.2 | async-start | bytes 98304 | tf_op jit(solution)/shard_map/all_to_all | solution.py:152
  25.5 0.1 copy.276
  25.6 0.1 reshape.2162
  25.7 0.6 gather_fusion.1
  26.3 0.6 copy-done.4
  26.9 0.7 %copy-done.6 = f32[24]{0:T(128)S(1)} copy-done((f32[24]{0:T(128)S(1)}, f32[24]{0:T(128)}, u32[]{:S(2)}) %copy-start.6) | copy-done | bytes 120
  27.6 0.3 fusion.91
  27.9 0.3 fusion.93
  28.3 0.3 fusion.95
  28.6 0.3 copy-done.5
  29.1 0.1 copy.274
  29.1 2.0 %all-to-all-done.2 = f32[4,4,2,3,128]{4,2,1,3,0:T(2,128)S(1)} async-done(((f32[4,4,2,3,128]{4,2,1,3,0:T(2,128)}), f32[4,4,2,3,128]{4,2,1,3,0:T(2,128)S(1)}, u32[]{:S(2)}, u32[]{:S(2)}) %all-to-all-start.2) | async-done | bytes 49184 | tf_op jit(solution)/shard_map/all_to_all | solution.py:152
  31.1 0.6 copy.282
  31.8 3.3 %all-to-all-start.3 = ((f32[4,4,2,3,128]{4,2,0,3,1:T(2,128)}), f32[4,4,2,3,128]{4,2,0,3,1:T(2,128)S(1)}, u32[]{:S(2)}, u32[]{:S(2)}) async-start(f32[4,4,2,3,128]{4,2,0,3,1:T(2,128)} %copy.282), calls=%async_computation.3 | async-start | bytes 98304 | tf_op jit(solution)/shard_map/all_to_all | solution.py:151
  35.2 0.7 %gather_fusion = f32[32,4,512]{2,1,0:T(4,128)S(1)} fusion(f32[64,4,512]{2,1,0:T(4,128)S(1)} %copy-done, s32[1024]{0:T(1024)S(1)} %pad_clamp_fusion.1), kind=kCustom, calls=%fused_computation | custom fusion | bytes 524416 | tf_op jit(solution)/shard_map/gather | solution.py:181
  35.9 0.2 reshape.2163
  36.1 0.1 copy.275
  36.2 2.8 %all-to-all-done.3 = f32[4,4,2,3,128]{4,2,0,3,1:T(2,128)S(1)} async-done(((f32[4,4,2,3,128]{4,2,0,3,1:T(2,128)}), f32[4,4,2,3,128]{4,2,0,3,1:T(2,128)S(1)}, u32[]{:S(2)}, u32[]{:S(2)}) %all-to-all-start.3) | async-done | bytes 49184 | tf_op jit(solution)/shard_map/all_to_all | solution.py:151
  39.1 0.3 convolution_subtract_fusion
  39.7 0.6 copy-done.2
  40.5 0.3 fusion.23
  40.9 0.3 fusion.17
  41.4 0.3 fusion.19
  41.7 0.3 fusion.21
  42.5 0.3 fusion.13
  42.9 0.3 fusion.11
  43.3 0.3 fusion.15
  43.7 0.3 fusion.9
  44.3 0.1 broadcast_add_fusion.2
  44.4 1.1 %fusion.4 = (f32[32,8,128]{2,1,0:T(8,128)S(1)}, f32[32,8,128]{2,1,0:T(8,128)S(1)}, f32[32,8,128]{2,1,0:T(8,128)S(1)}) fusion(f32[32,8,128]{2,1,0:T(8,128)S(1)} %get-tuple-element.61, f32[8,8]{1,0:T(8,128)S(1)} %add_add_fusion, pred[8,8]{1,0:T(8,128)(4,1)S(1)} %iota_compare_fusion.1, f32[32,8,128]{2,1,0:T(8,128)S(1)} %get-tuple-element.60, ...), kind=kLoop, calls=%fused_computation.14 | loop fusion | flops 2260992 | bytes 786752 | tf_op jit(solution)/shard_map/vmap()/reduce_prod | solution.py:28
  45.4 1.1 %fusion.1 = f32[32,4,128]{2,1,0:T(4,128)S(1)} fusion(f32[32,32,64]{2,1,0:T(8,128)S(1)} %reshape.2163, f32[32,8,128]{2,1,0:T(8,128)S(1)} %get-tuple-element.6, f32[32,8,128]{2,1,0:T(8,128)S(1)} %get-tuple-element.7, f32[32,8,128]{2,1,0:T(8,128)S(1)} %get-tuple-element.5), kind=kOutput, calls=%fused_computation.7 | convolution fusion | flops 101171200 | bytes 720896 | tf_op jit(solution)/shard_map/vmap()/dot_general | solution.py:114
  46.6 0.1 broadcast_select_fusion
  46.7 8.6 %all_to_all.30 = f32[4,4,2,4,128]{4,2,1,3,0:T(2,128)S(1)} all-to-all(f32[4,4,2,4,128]{4,2,1,3,0:T(2,128)S(1)} %copy.319), channel_id=1, replica_groups=mesh['groups'=2,'block'=4,'seg'=2,'sub'=2] {'block'}, dimensions={0} | all-to-all | bytes 131072 | tf_op jit(solution)/shard_map/all_to_all | solution.py:186
  55.3 0.6 %copy.320 = f32[4,4,2,4,128]{4,3,2,0,1:T(4,128)} copy(f32[4,4,2,4,128]{4,2,1,3,0:T(2,128)S(1)} %all_to_all.30) | data formatting | bytes 131072 | tf_op jit(solution)/shard_map/all_to_all | solution.py:186
  56.0 3.3 %all-to-all-start.5 = ((f32[4,4,2,4,128]{4,3,2,0,1:T(4,128)}), f32[4,4,2,4,128]{4,3,2,0,1:T(4,128)S(1)}, u32[]{:S(2)}, u32[]{:S(2)}) async-start(f32[4,4,2,4,128]{4,3,2,0,1:T(4,128)} %copy.320), calls=%async_computation.5 | async-start | bytes 131072 | tf_op jit(solution)/shard_map/all_to_all | solution.py:185
  59.3 4.1 %all-to-all-done.5 = f32[4,4,2,4,128]{4,3,2,0,1:T(4,128)S(1)} async-done(((f32[4,4,2,4,128]{4,3,2,0,1:T(4,128)}), f32[4,4,2,4,128]{4,3,2,0,1:T(4,128)S(1)}, u32[]{:S(2)}, u32[]{:S(2)}) %all-to-all-start.5) | async-done | bytes 65568 | tf_op jit(solution)/shard_map/all_to_all | solution.py:185
  63.4 1.2 %gather_fusion.2 = f32[32,4,128]{2,1,0:T(4,128)} fusion(f32[32,4,128]{2,1,0:T(4,128)S(1)} %bitcast.769, s32[1024]{0:T(1024)S(1)} %pad_clamp_fusion), kind=kCustom, calls=%fused_computation.2 | custom fusion | bytes 131200 | tf_op jit(solution)/shard_map/gather | solution.py:198
  (75 shorter events, 1.7 us)
Async XLA Ops:
  0.0 35.1 %copy-start = (f32[64,4,512]{2,1,0:T(4,128)S(1)}, f32[64,4,512]{2,1,0:T(4,128)}, u32[]{:S(2)}) copy-start(f32[64,4,512]{2,1,0:T(4,128)} %param.8) | copy-start | bytes 1572868
  1.7 7.2 %copy-start.3 = (f32[24,64]{1,0:T(8,128)S(1)}, f32[24,64]{1,0:T(8,128)}, u32[]{:S(2)}) copy-start(f32[24,64]{1,0:T(8,128)} %param.9) | copy-start | bytes 18436
  1.7 7.3 %copy-start.7 = (f32[8]{0:T(128)S(1)}, f32[8]{0:T(128)}, u32[]{:S(2)}) copy-start(f32[8]{0:T(128)} %constant.77) | copy-start | bytes 100
  1.7 7.3 %copy-start.8 = (f32[8]{0:T(128)S(1)}, f32[8]{0:T(128)}, u32[]{:S(2)}) copy-start(f32[8]{0:T(128)} %constant.75.clone) | copy-start | bytes 100
  2.4 6.7 %copy-start.1 = (f32[3,4096]{1,0:T(4,128)S(1)}, f32[3,4096]{1,0:T(4,128)}, u32[]{:S(2)}) copy-start(f32[3,4096]{1,0:T(4,128)} %param.10) | copy-start | bytes 147460
  2.4 12.1 %all-to-all-start = ((s32[4,4,2]{1,2,0:T(2,128)}), s32[4,4,2]{1,2,0:T(2,128)S(1)}, u32[]{:S(2)}, u32[]{:S(2)}) async-start(s32[4,4,2]{1,2,0:T(2,128)} %copy.272), calls=%async_computation | async-start | bytes 8192 | tf_op jit(solution)/shard_map/all_to_all | solution.py:165
  15.2 7.0 %all-to-all-start.1 = ((s32[4,4,2]{0,2,1:T(2,128)}), s32[4,4,2]{0,2,1:T(2,128)S(1)}, u32[]{:S(2)}, u32[]{:S(2)}) async-start(s32[4,4,2]{0,2,1:T(2,128)} %copy.273), calls=%async_computation.1 | async-start | bytes 8192 | tf_op jit(solution)/shard_map/all_to_all | solution.py:164
  22.2 8.9 %all-to-all-start.2 = ((f32[4,4,2,3,128]{4,2,1,3,0:T(2,128)}), f32[4,4,2,3,128]{4,2,1,3,0:T(2,128)S(1)}, u32[]{:S(2)}, u32[]{:S(2)}) async-start(f32[4,4,2,3,128]{4,2,1,3,0:T(2,128)} %copy.281), calls=%async_computation.2 | async-start | bytes 98304 | tf_op jit(solution)/shard_map/all_to_all | solution.py:152
  26.3 0.7 %copy-start.4 = (f32[2,128]{1,0:T(2,128)S(1)}, f32[2,128]{1,0:T(2,128)}, u32[]{:S(2)}) copy-start(f32[2,128]{1,0:T(2,128)} %constant.68.clone.1) | copy-start | bytes 3076
  26.9 0.7 %copy-start.6 = (f32[24]{0:T(128)S(1)}, f32[24]{0:T(128)}, u32[]{:S(2)}) copy-start(f32[24]{0:T(128)} %constant.76) | copy-start | bytes 292
  28.3 0.7 %copy-start.5 = (f32[3,8]{1,0:T(4,128)S(1)}, f32[3,8]{1,0:T(4,128)}, u32[]{:S(2)}) copy-start(f32[3,8]{1,0:T(4,128)} %constant.74.clone) | copy-start | bytes 292
  31.8 7.3 %all-to-all-start.3 = ((f32[4,4,2,3,128]{4,2,0,3,1:T(2,128)}), f32[4,4,2,3,128]{4,2,0,3,1:T(2,128)S(1)}, u32[]{:S(2)}, u32[]{:S(2)}) async-start(f32[4,4,2,3,128]{4,2,0,3,1:T(2,128)} %copy.282), calls=%async_computation.3 | async-start | bytes 98304 | tf_op jit(solution)/shard_map/all_to_all | solution.py:151
  39.6 0.7 %copy-start.2 = (f32[2,128]{1,0:T(2,128)S(1)}, f32[2,128]{1,0:T(2,128)}, u32[]{:S(2)}) copy-start(f32[2,128]{1,0:T(2,128)} %constant.73.clone.1) | copy-start | bytes 3076
  56.0 7.4 %all-to-all-start.5 = ((f32[4,4,2,4,128]{4,3,2,0,1:T(4,128)}), f32[4,4,2,4,128]{4,3,2,0,1:T(4,128)S(1)}, u32[]{:S(2)}, u32[]{:S(2)}) async-start(f32[4,4,2,4,128]{4,3,2,0,1:T(4,128)} %copy.320), calls=%async_computation.5 | async-start | bytes 131072 | tf_op jit(solution)/shard_map/all_to_all | solution.py:185
where the time goes:
time: 65.3 us; the launch traced here: 64.6 us
  starting transfers between devices  19.6 us (30%)
  waiting for transfers between devices  15.9 us (24%)
  local copies, waits for them, and re-layouts  12 us (18%)
  blocking collectives  8.63 us (13%)
  matrix products  5.16 us (8%)
  other arithmetic  2.71 us (4%)
    all_to_all x1, blocking collectives, shards(): lax.all_to_all(computed.reshape(outer_count, inner_count, CAP, var_count,...  8.63 us
    all_to_all x1, starting transfers between devices, shards(): lax.all_to_all(wanted.reshape(outer_count, inner_count, CAP), 'block', sp...  6.48 us
    all_to_all x1, waiting for transfers between devices, shards(): lax.all_to_all(lax.all_to_all(computed.reshape(outer_count, inner_count,...  4.07 us
    all_to_all x1, waiting for transfers between devices, shards(): lax.all_to_all(wanted.reshape(outer_count, inner_count, CAP), 'block', sp...  3.88 us
    all_to_all x1, starting transfers between devices, shards(): lax.all_to_all(lax.all_to_all(computed.reshape(outer_count, inner_count,...  3.28 us
    all_to_all x1, starting transfers between devices, shards(): lax.all_to_all(outgoing.reshape(outer_count, inner_count, CAP, 3, point_c...  3.27 us
    all_to_all x1, starting transfers between devices, shards(): lax.all_to_all(lax.all_to_all(outgoing.reshape(outer_count, inner_count,...  3.27 us
    all_to_all x1, starting transfers between devices, shards(): lax.all_to_all(lax.all_to_all(wanted.reshape(outer_count, inner_count, CA...  3.24 us
  transfers between devices with their start and end apart: 5, of which 5 were waited for; matrix products, arithmetic and copies ran while one was open for 8% of the time, Pallas kernels for 0%

commit v1 on v0

--- a/solution.py
+++ b/solution.py
@@ -17,6 +17,28 @@
     1.0,
 )
 EXACT = lax.Precision.HIGHEST
+
+
+def split_up(x, dim, size):
+    before, after = (x.shape[:dim], x.shape[dim + 1 :])
+    return jnp.moveaxis(x.reshape(*before, size, -1, *after), dim, 0)
+
+
+def laid_out(blocks, dim):
+    blocks = jnp.moveaxis(blocks, 0, dim)
+    shape = blocks.shape
+    return blocks.reshape(*shape[:dim], shape[dim] * shape[dim + 1], *shape[dim + 2 :])
+
+
+def exchange_in_pairs(shard, axis, split_dim, concat_dim):
+    size, index = (lax.axis_size(axis), lax.axis_index(axis))
+    tiles = split_up(shard, split_dim, size)
+    outs = [tiles[index]]
+    for step in range(1, size):
+        sent = tiles[index ^ step]
+        outs.append(lax.ppermute(sent, axis, [(i, i ^ step) for i in range(size)]))
+    tiles = jnp.stack(outs)[index ^ jnp.arange(size)]
+    return laid_out(tiles, concat_dim)
 
 
 def lagrange_rows(coords):
@@ -182,7 +204,7 @@
     shifts = jnp.transpose(corner_shift[:, element])
     computed = interpolate_blocks(fields, shifts, arrived.reshape(slot_count, 3, point_count))
     computed = jnp.where(live_slot[:, None, None], computed, 0.0)
-    returned = lax.all_to_all(
+    returned = exchange_in_pairs(
         lax.all_to_all(
             computed.reshape(outer_count, inner_count, CAP, var_count, point_count),
             "block",
@@ -191,9 +213,8 @@
             tiled=True,
         ),
         ("seg", "sub"),
-        split_axis=1,
-        concat_axis=1,
-        tiled=True,
+        1,
+        1,
     )
     mine = returned.reshape(slot_count, var_count, point_count)[slot_index]
     return mine.transpose(1, 0, 2).reshape(var_count, -1)

time: 65.3 us -> 62.7 us (0.960)
  blocking collectives: 8.63 us -> 0 us
  waiting for transfers between devices: 15.9 us -> 18.7 us
  starting transfers between devices: 19.6 us -> 21.3 us
  local copies, waits for them, and re-layouts: 12 us -> 13.4 us
    all_to_all x1 -> x0, blocking collectives: 8.63 us -> none  [shards(): lax.all_to_all(computed.reshape(outer_count, inner_count, CAP, var_count,...]
    ppermute x0 -> x3, waiting for transfers between devices: none -> 1.95 us  [exchange_in_pairs(): outs.append(lax.ppermute(sent, axis, [(i, i ^ step) for i in range(size)]))]
    ppermute x0 -> x3, starting transfers between devices: none -> 1.92 us  [exchange_in_pairs(): outs.append(lax.ppermute(sent, axis, [(i, i ^ step) for i in range(size)]))]
    all_to_all x1, waiting for transfers between devices: 4.07 us -> 5.7 us  [shards(): lax.all_to_all(computed.reshape(outer_count, inner_count, CAP, var_count,...]
    all_to_all x1, waiting for transfers between devices: 3.88 us -> 2.47 us  [shards(): lax.all_to_all(wanted.reshape(outer_count, inner_count, CAP), 'block', sp...]
    unnamed x19, local copies, waits for them, and re-layouts: 2.35 us -> 3.06 us
    select_n x1, local copies, waits for them, and re-layouts: 0.01 us -> 0.67 us  [shards(): computed = jnp.where(live_slot[:, None, None], computed, 0.0)]
  transfers between devices with their start and end apart: 5 -> 8, of which waited for: 5 -> 6; matrix products, arithmetic and copies ran while one was open for 8% -> 9% of each run, Pallas kernels for 0% -> 0%
where the time goes in v1:
time: 62.7 us; the launch traced here: 62 us
  starting transfers between devices  21.3 us (34%)
  waiting for transfers between devices  18.7 us (30%)
  local copies, waits for them, and re-layouts  13.4 us (21%)
  matrix products  5.16 us (8%)
  other arithmetic  2.74 us (4%)
  between operations  0.68 us (1%)
    all_to_all x1, starting transfers between devices, shards(): lax.all_to_all(wanted.reshape(outer_count, inner_count, CAP), 'block', sp...  6.35 us
    all_to_all x1, waiting for transfers between devices, shards(): lax.all_to_all(computed.reshape(outer_count, inner_count, CAP, var_count,...  5.7 us
    all_to_all x1, waiting for transfers between devices, shards(): lax.all_to_all(lax.all_to_all(wanted.reshape(outer_count, inner_count, CA...  3.76 us
    all_to_all x1, starting transfers between devices, shards(): lax.all_to_all(computed.reshape(outer_count, inner_count, CAP, var_count,...  3.28 us
    all_to_all x1, starting transfers between devices, shards(): lax.all_to_all(outgoing.reshape(outer_count, inner_count, CAP, 3, point_c...  3.27 us
    all_to_all x1, starting transfers between devices, shards(): lax.all_to_all(lax.all_to_all(outgoing.reshape(outer_count, inner_count,...  3.27 us
    all_to_all x1, starting transfers between devices, shards(): lax.all_to_all(lax.all_to_all(wanted.reshape(outer_count, inner_count, CA...  3.2 us
    unnamed x19, local copies, waits for them, and re-layouts  3.06 us
  transfers between devices with their start and end apart: 8, of which 6 were waited for; matrix products, arithmetic and copies ran while one was open for 9% of the time, Pallas kernels for 0%

profile of v1, /device:TPU:0, one launch (start us, length us, event | category | flops | bytes accessed | tf_op | source)
XLA Modules:
  0.0 62.0 jit_solution(17651697479478082455)
XLA Ops:
  0.0 0.7 %multiply_subtract_fusion.2 = (s32[32]{0:T(128)S(1)}, s32[32]{0:T(128)S(1)}, s32[32]{0:T(128)S(1)}) fusion(s32[32]{0:T(128)} %param.11), kind=kLoop, calls=%fused_computation.246 | loop fusion | flops 576 | bytes 512 | tf_op jit(solution)/shard_map/sub | solution.py:152
  0.7 0.2 select_reduce_fusion
  0.9 0.7 %scatter_custom_fusion = s32[32]{0:T(128)S(1)} fusion(s32[32]{0:T(128)S(1)} %compare_select_fusion.3, s32[32]{0:T(128)S(1)} %get-tuple-element.10, s32[]{:T(128)} %constant.29.clone.1), kind=kCustom, calls=%fused_computation.248 | custom fusion | bytes 132 | tf_op jit(solution)/shard_map/scatter | solution.py:171
  1.7 0.7 %copy.279 = s32[4,4,2]{1,2,0:T(2,128)} copy(s32[4,4,2]{2,1,0:T(4,128)S(1)} %reshape.2190) | data formatting | bytes 256 | tf_op jit(solution)/shard_map/reshape | solution.py:188
  2.4 6.3 %all-to-all-start = ((s32[4,4,2]{1,2,0:T(2,128)}), s32[4,4,2]{1,2,0:T(2,128)S(1)}, u32[]{:S(2)}, u32[]{:S(2)}) async-start(s32[4,4,2]{1,2,0:T(2,128)} %copy.279), calls=%async_computation | async-start | bytes 8192 | tf_op jit(solution)/shard_map/all_to_all | solution.py:187
  8.8 0.7 %copy-done.3 = f32[24,64]{1,0:T(8,128)S(1)} copy-done((f32[24,64]{1,0:T(8,128)S(1)}, f32[24,64]{1,0:T(8,128)}, u32[]{:S(2)}) %copy-start.3) | copy-done | bytes 6168
  9.6 1.5 %scatter_fusion = f32[32,3,128]{2,1,0:T(4,128)S(1)} fusion(f32[32,3,128]{2,1,0:T(4,128)S(1)} %broadcast.596, s32[32]{0:T(128)S(1)} %compare_select_fusion.3, f32[32,3,128]{2,1,0:T(4,128)S(1)} %bitcast.809), kind=kCustom, calls=%fused_computation.5 | custom fusion | bytes 147584 | tf_op jit(solution)/shard_map/scatter | solution.py:170
  11.1 0.6 %copy.288 = f32[4,4,2,3,128]{4,2,1,3,0:T(2,128)} copy(f32[4,4,2,3,128]{4,3,2,1,0:T(4,128)S(1)} %bitcast.785) | data formatting | bytes 98304 | tf_op jit(solution)/shard_map/reshape | solution.py:175
  11.9 2.5 %all-to-all-done = s32[4,4,2]{1,2,0:T(2,128)S(1)} async-done(((s32[4,4,2]{1,2,0:T(2,128)}), s32[4,4,2]{1,2,0:T(2,128)S(1)}, u32[]{:S(2)}, u32[]{:S(2)}) %all-to-all-start) | async-done | bytes 160 | tf_op jit(solution)/shard_map/all_to_all | solution.py:187
  14.3 0.7 %copy.280 = s32[4,4,2]{0,2,1:T(2,128)} copy(s32[4,4,2]{1,2,0:T(2,128)S(1)} %all-to-all-done) | data formatting | bytes 256 | tf_op jit(solution)/shard_map/all_to_all | solution.py:187
  15.0 3.2 %all-to-all-start.1 = ((s32[4,4,2]{0,2,1:T(2,128)}), s32[4,4,2]{0,2,1:T(2,128)S(1)}, u32[]{:S(2)}, u32[]{:S(2)}) async-start(s32[4,4,2]{0,2,1:T(2,128)} %copy.280), calls=%async_computation.1 | async-start | bytes 8192 | tf_op jit(solution)/shard_map/all_to_all | solution.py:186
  18.2 3.8 %all-to-all-done.1 = s32[4,4,2]{0,2,1:T(2,128)S(1)} async-done(((s32[4,4,2]{0,2,1:T(2,128)}), s32[4,4,2]{0,2,1:T(2,128)S(1)}, u32[]{:S(2)}, u32[]{:S(2)}) %all-to-all-start.1) | async-done | bytes 160 | tf_op jit(solution)/shard_map/all_to_all | solution.py:186
  22.0 3.3 %all-to-all-start.2 = ((f32[4,4,2,3,128]{4,2,1,3,0:T(2,128)}), f32[4,4,2,3,128]{4,2,1,3,0:T(2,128)S(1)}, u32[]{:S(2)}, u32[]{:S(2)}) async-start(f32[4,4,2,3,128]{4,2,1,3,0:T(2,128)} %copy.288), calls=%async_computation.2 | async-start | bytes 98304 | tf_op jit(solution)/shard_map/all_to_all | solution.py:174
  25.3 0.1 copy.283
  25.5 0.6 gather_fusion.1
  26.1 0.6 copy-done.4
  26.8 0.7 %copy-done.6 = f32[24]{0:T(128)S(1)} copy-done((f32[24]{0:T(128)S(1)}, f32[24]{0:T(128)}, u32[]{:S(2)}) %copy-start.6) | copy-done | bytes 120
  27.4 0.3 fusion.91
  27.8 0.3 fusion.93
  28.1 0.3 fusion.95
  28.4 0.3 copy-done.5
  29.0 2.0 %all-to-all-done.2 = f32[4,4,2,3,128]{4,2,1,3,0:T(2,128)S(1)} async-done(((f32[4,4,2,3,128]{4,2,1,3,0:T(2,128)}), f32[4,4,2,3,128]{4,2,1,3,0:T(2,128)S(1)}, u32[]{:S(2)}, u32[]{:S(2)}) %all-to-all-start.2) | async-done | bytes 49184 | tf_op jit(solution)/shard_map/all_to_all | solution.py:174
  30.9 0.6 %copy.289 = f32[4,4,2,3,128]{4,2,0,3,1:T(2,128)} copy(f32[4,4,2,3,128]{4,2,1,3,0:T(2,128)S(1)} %all-to-all-done.2) | data formatting | bytes 98304 | tf_op jit(solution)/shard_map/all_to_all | solution.py:174
  31.6 3.3 %all-to-all-start.3 = ((f32[4,4,2,3,128]{4,2,0,3,1:T(2,128)}), f32[4,4,2,3,128]{4,2,0,3,1:T(2,128)S(1)}, u32[]{:S(2)}, u32[]{:S(2)}) async-start(f32[4,4,2,3,128]{4,2,0,3,1:T(2,128)} %copy.289), calls=%async_computation.3 | async-start | bytes 98304 | tf_op jit(solution)/shard_map/all_to_all | solution.py:173
  35.0 0.7 %gather_fusion = f32[32,4,512]{2,1,0:T(4,128)S(1)} fusion(f32[64,4,512]{2,1,0:T(4,128)S(1)} %copy-done, s32[1024]{0:T(1024)S(1)} %pad_clamp_fusion.2), kind=kCustom, calls=%fused_computation | custom fusion | bytes 524416 | tf_op jit(solution)/shard_map/gather | solution.py:203
  35.7 0.2 reshape.2192
  35.9 0.1 copy.282
  36.0 2.8 %all-to-all-done.3 = f32[4,4,2,3,128]{4,2,0,3,1:T(2,128)S(1)} async-done(((f32[4,4,2,3,128]{4,2,0,3,1:T(2,128)}), f32[4,4,2,3,128]{4,2,0,3,1:T(2,128)S(1)}, u32[]{:S(2)}, u32[]{:S(2)}) %all-to-all-start.3) | async-done | bytes 49184 | tf_op jit(solution)/shard_map/all_to_all | solution.py:173
  38.9 0.3 convolution_subtract_fusion
  39.5 0.6 %copy-done.2 = f32[2,128]{1,0:T(2,128)S(1)} copy-done((f32[2,128]{1,0:T(2,128)S(1)}, f32[2,128]{1,0:T(2,128)}, u32[]{:S(2)}) %copy-start.2) | copy-done | bytes 1048
  40.3 0.3 fusion.23
  40.7 0.3 fusion.17
  41.2 0.3 fusion.19
  41.5 0.3 fusion.21
  42.3 0.3 fusion.13
  42.7 0.3 fusion.11
  43.1 0.3 fusion.15
  43.5 0.3 fusion.9
  44.2 1.1 %fusion.4 = (f32[32,8,128]{2,1,0:T(8,128)S(1)}, f32[32,8,128]{2,1,0:T(8,128)S(1)}, f32[32,8,128]{2,1,0:T(8,128)S(1)}) fusion(f32[32,8,128]{2,1,0:T(8,128)S(1)} %get-tuple-element.65, f32[8,8]{1,0:T(8,128)S(1)} %add_add_fusion, pred[8,8]{1,0:T(8,128)(4,1)S(1)} %iota_compare_fusion.1, f32[32,8,128]{2,1,0:T(8,128)S(1)} %get-tuple-element.64, ...), kind=kLoop, calls=%fused_computation.15 | loop fusion | flops 2260992 | bytes 786752 | tf_op jit(solution)/shard_map/vmap()/reduce_prod | solution.py:50
  45.2 1.1 %fusion.1 = f32[32,4,128]{2,1,0:T(4,128)S(1)} fusion(f32[32,32,64]{2,1,0:T(8,128)S(1)} %reshape.2192, f32[32,8,128]{2,1,0:T(8,128)S(1)} %get-tuple-element.6, f32[32,8,128]{2,1,0:T(8,128)S(1)} %get-tuple-element.7, f32[32,8,128]{2,1,0:T(8,128)S(1)} %get-tuple-element.5), kind=kOutput, calls=%fused_computation.8 | convolution fusion | flops 101171200 | bytes 720896 | tf_op jit(solution)/shard_map/vmap()/dot_general | solution.py:136
  46.5 0.7 %copy.326 = f32[4,4,2,4,128]{4,3,2,1,0:T(4,128)} copy(f32[4,4,2,4,128]{4,2,1,0,3:T(2,128)S(1)} %broadcast_select_fusion) | data formatting | bytes 131072 | tf_op jit(solution)/shard_map/jit(_where)/select_n | solution.py:206
  47.2 3.3 %all-to-all-start.4 = ((f32[4,4,2,4,128]{4,3,2,1,0:T(4,128)}), f32[4,4,2,4,128]{4,3,2,1,0:T(4,128)S(1)}, u32[]{:S(2)}, u32[]{:S(2)}) async-start(f32[4,4,2,4,128]{4,3,2,1,0:T(4,128)} %copy.326), calls=%async_computation.4 | async-start | bytes 131072 | tf_op jit(solution)/shard_map/all_to_all | solution.py:208
  50.5 5.7 %all-to-all-done.4 = f32[4,4,2,4,128]{4,3,2,1,0:T(4,128)S(1)} async-done(((f32[4,4,2,4,128]{4,3,2,1,0:T(4,128)}), f32[4,4,2,4,128]{4,3,2,1,0:T(4,128)S(1)}, u32[]{:S(2)}, u32[]{:S(2)}) %all-to-all-start.4) | async-done | bytes 65568 | tf_op jit(solution)/shard_map/all_to_all | solution.py:208
  56.3 0.1 collective-permute-start.1
  56.4 1.7 %collective-permute-start.2 = (f32[4,1,2,4,128]{4,3,2,0,1:T(4,128)S(1)}, f32[4,1,2,4,128]{4,3,2,0,1:T(4,128)S(1)}, u32[]{:S(2)}, u32[]{:S(2)}) collective-permute-start(f32[4,1,2,4,128]{4,3,2,0,1:T(4,128)S(1)} %get-tuple-element.23), channel_id=1, source_target_pairs={{0,3},{1,2},{2,1},{3,0},{4,7},{5,6},{6,5},{7,4},{8,11},{9,10},{10,... | collective-permute-start | bytes 49160 | tf_op jit(solution)/shard_map/ppermute | solution.py:39
  58.1 1.9 %collective-permute-done.1 = f32[4,1,2,4,128]{4,3,2,0,1:T(4,128)S(1)} collective-permute-done((f32[4,1,2,4,128]{4,3,2,0,1:T(4,128)S(1)}, f32[4,1,2,4,128]{4,3,2,0,1:T(4,128)S(1)}, u32[]{:S(2)}, u32[]{:S(2)}) %collective-permute-start.1) | collective-permute-done | bytes 16416 | tf_op jit(solution)/shard_map/ppermute | solution.py:39
  60.1 0.6 gather_fusion.2
  60.8 1.2 %gather_fusion.3 = f32[32,4,128]{2,1,0:T(4,128)} fusion(f32[32,4,128]{2,1,0:T(4,128)S(1)} %copy.331, s32[1024]{0:T(1024)S(1)} %pad_clamp_fusion), kind=kCustom, calls=%fused_computation.3 | custom fusion | bytes 131200 | tf_op jit(solution)/shard_map/gather | solution.py:219
  (85 shorter events, 2.3 us)
Async XLA Ops:
  0.0 35.0 %copy-start = (f32[64,4,512]{2,1,0:T(4,128)S(1)}, f32[64,4,512]{2,1,0:T(4,128)}, u32[]{:S(2)}) copy-start(f32[64,4,512]{2,1,0:T(4,128)} %param.8) | copy-start | bytes 1572868
  2.4 11.9 %all-to-all-start = ((s32[4,4,2]{1,2,0:T(2,128)}), s32[4,4,2]{1,2,0:T(2,128)S(1)}, u32[]{:S(2)}, u32[]{:S(2)}) async-start(s32[4,4,2]{1,2,0:T(2,128)} %copy.279), calls=%async_computation | async-start | bytes 8192 | tf_op jit(solution)/shard_map/all_to_all | solution.py:187
  8.8 0.7 %copy-start.3 = (f32[24,64]{1,0:T(8,128)S(1)}, f32[24,64]{1,0:T(8,128)}, u32[]{:S(2)}) copy-start(f32[24,64]{1,0:T(8,128)} %param.9) | copy-start | bytes 18436
  8.8 0.8 %copy-start.1 = (f32[3,4096]{1,0:T(4,128)S(1)}, f32[3,4096]{1,0:T(4,128)}, u32[]{:S(2)}) copy-start(f32[3,4096]{1,0:T(4,128)} %param.10) | copy-start | bytes 147460
  11.1 0.7 %copy-start.7 = (f32[8]{0:T(128)S(1)}, f32[8]{0:T(128)}, u32[]{:S(2)}) copy-start(f32[8]{0:T(128)} %constant.91) | copy-start | bytes 100
  11.1 0.7 %copy-start.8 = (f32[8]{0:T(128)S(1)}, f32[8]{0:T(128)}, u32[]{:S(2)}) copy-start(f32[8]{0:T(128)} %constant.89.clone) | copy-start | bytes 100
  15.0 7.0 %all-to-all-start.1 = ((s32[4,4,2]{0,2,1:T(2,128)}), s32[4,4,2]{0,2,1:T(2,128)S(1)}, u32[]{:S(2)}, u32[]{:S(2)}) async-start(s32[4,4,2]{0,2,1:T(2,128)} %copy.280), calls=%async_computation.1 | async-start | bytes 8192 | tf_op jit(solution)/shard_map/all_to_all | solution.py:186
  22.0 8.9 %all-to-all-start.2 = ((f32[4,4,2,3,128]{4,2,1,3,0:T(2,128)}), f32[4,4,2,3,128]{4,2,1,3,0:T(2,128)S(1)}, u32[]{:S(2)}, u32[]{:S(2)}) async-start(f32[4,4,2,3,128]{4,2,1,3,0:T(2,128)} %copy.288), calls=%async_computation.2 | async-start | bytes 98304 | tf_op jit(solution)/shard_map/all_to_all | solution.py:174
  26.1 0.7 %copy-start.4 = (f32[2,128]{1,0:T(2,128)S(1)}, f32[2,128]{1,0:T(2,128)}, u32[]{:S(2)}) copy-start(f32[2,128]{1,0:T(2,128)} %constant.79.clone.1) | copy-start | bytes 3076
  26.8 0.7 %copy-start.6 = (f32[24]{0:T(128)S(1)}, f32[24]{0:T(128)}, u32[]{:S(2)}) copy-start(f32[24]{0:T(128)} %constant.90) | copy-start | bytes 292
  28.1 0.7 %copy-start.5 = (f32[3,8]{1,0:T(4,128)S(1)}, f32[3,8]{1,0:T(4,128)}, u32[]{:S(2)}) copy-start(f32[3,8]{1,0:T(4,128)} %constant.88.clone) | copy-start | bytes 292
  31.6 7.3 %all-to-all-start.3 = ((f32[4,4,2,3,128]{4,2,0,3,1:T(2,128)}), f32[4,4,2,3,128]{4,2,0,3,1:T(2,128)S(1)}, u32[]{:S(2)}, u32[]{:S(2)}) async-start(f32[4,4,2,3,128]{4,2,0,3,1:T(2,128)} %copy.289), calls=%async_computation.3 | async-start | bytes 98304 | tf_op jit(solution)/shard_map/all_to_all | solution.py:173
  39.4 0.7 %copy-start.2 = (f32[2,128]{1,0:T(2,128)S(1)}, f32[2,128]{1,0:T(2,128)}, u32[]{:S(2)}) copy-start(f32[2,128]{1,0:T(2,128)} %constant.84.clone.1) | copy-start | bytes 3076
  47.2 9.0 %all-to-all-start.4 = ((f32[4,4,2,4,128]{4,3,2,1,0:T(4,128)}), f32[4,4,2,4,128]{4,3,2,1,0:T(4,128)S(1)}, u32[]{:S(2)}, u32[]{:S(2)}) async-start(f32[4,4,2,4,128]{4,3,2,1,0:T(4,128)} %copy.326), calls=%async_computation.4 | async-start | bytes 131072 | tf_op jit(solution)/shard_map/all_to_all | solution.py:208
  56.2 1.9 %collective-permute-start = (f32[4,1,2,4,128]{4,3,2,0,1:T(4,128)S(1)}, f32[4,1,2,4,128]{4,3,2,0,1:T(4,128)S(1)}, u32[]{:S(2)}, u32[]{:S(2)}) collective-permute-start(f32[4,1,2,4,128]{4,3,2,0,1:T(4,128)S(1)} %get-tuple-element.22), channel_id=1, source_target_pairs={{0,1},{1,0},{2,3},{3,2},{4,5},{5,4},{6,7},{7,6},{8,9},{9,8},{10,11... | collective-permute-start | bytes 49160 | tf_op jit(solution)/shard_map/ppermute | solution.py:39
  56.3 3.8 %collective-permute-start.1 = (f32[4,1,2,4,128]{4,3,2,0,1:T(4,128)S(1)}, f32[4,1,2,4,128]{4,3,2,0,1:T(4,128)S(1)}, u32[]{:S(2)}, u32[]{:S(2)}) collective-permute-start(f32[4,1,2,4,128]{4,3,2,0,1:T(4,128)S(1)} %get-tuple-element.21), channel_id=1, source_target_pairs={{0,2},{1,3},{2,0},{3,1},{4,6},{5,7},{6,4},{7,5},{8,10},{9,11},{10,... | collective-permute-start | bytes 49160 | tf_op jit(solution)/shard_map/ppermute | solution.py:39
  56.4 3.7 %collective-permute-start.2 = (f32[4,1,2,4,128]{4,3,2,0,1:T(4,128)S(1)}, f32[4,1,2,4,128]{4,3,2,0,1:T(4,128)S(1)}, u32[]{:S(2)}, u32[]{:S(2)}) collective-permute-start(f32[4,1,2,4,128]{4,3,2,0,1:T(4,128)S(1)} %get-tuple-element.23), channel_id=1, source_target_pairs={{0,3},{1,2},{2,1},{3,0},{4,7},{5,6},{6,5},{7,4},{8,11},{9,10},{10,... | collective-permute-start | bytes 49160 | tf_op jit(solution)/shard_map/ppermute | solution.py:39
